TPU v7x, 512 devices: a whole 4x8x8 slice. The times are simulated.
512 devices in a mesh: layer: 16 (over x, y_lo), feat: 32 (over z, y_hi, core).
Axes of the slice: x: 4, y: 8 (y_hi: 2, y_lo: 4; y = y_hi * 4 + y_lo), z: 8, core: 2. Of those that a mesh axis runs over, the one named last changes fastest.
Arguments:
- acts: bfloat16 [16, 1024, 8192], P(None, 'layer', 'feat'), may hold values from -6 to 6
- layer_order: int32 [16, 16], P('layer'), may hold values from 0 to 15, each once within a row
- groups: int32 [8192], P('feat'), may hold values from 0 to 63
- group_scale: float32 [16, 64], P('layer'), may hold values from 0.25 to 4
- shrink: float32 [16], P('layer'), may hold values from 0.1 to 0.6
Outputs:
- factor_tiles: float32 [16, 32, 16, 256, 256], P('layer', 'feat')
- far_tiles: float32 [16, 32, 128, 256], P('layer', 'feat')
Inputs may be any that keep to these rules, and one draw needn't show every extreme that they name: Each row of layer_order names every layer once.
All inputs are finite; a program needn't handle non-finite values.
Results may differ from a plain program's by a relative error of at most 0.0003.
Values may be sent and summed in bfloat16 or wider, within the bound.
A program may use at most 64 MiB of HBM per device.

v0:
```python
import jax
import jax.numpy as jnp
from jax import lax
from jax.sharding import PartitionSpec as P


def shifted(block, axis, distance):
    devices = range(lax.axis_size(axis))
    route = [((i - distance) % len(devices), i) for i in devices]
    return lax.ppermute(block, axis, route)


def copy_for_each(value, axis):
    copies = jnp.broadcast_to(value, (lax.axis_size(axis), *value.shape))
    return lax.all_to_all(copies, axis, split_axis=0, concat_axis=0, tiled=True)


def of_everyone(value, axis):
    return copy_for_each(value, axis).sum(axis=0)


def product(left, right):
    return lax.dot_general(
        left, right, (((0,), (0,)), ((), ())), preferred_element_type=jnp.float32
    )


def shards(acts, layer_order, groups, group_scale, shrink):
    layers = acts.shape[0]
    pick = (layer_order[0][None, :] == jnp.arange(layers, dtype=jnp.int32)[:, None]).astype(
        jnp.bfloat16
    )
    ordered = jnp.einsum("ds,stc->dtc", pick, acts, preferred_element_type=jnp.float32).astype(
        jnp.bfloat16
    )
    gathered = lax.all_to_all(ordered, "layer", split_axis=0, concat_axis=1, tiled=True)
    panel = gathered[0]
    tokens = panel.shape[0]
    width = panel.shape[1]
    half = lax.axis_size("feat") // 2

    def advance(index, carry):
        moving, stack = carry
        stack = lax.dynamic_update_slice_in_dim(stack, product(panel, moving)[None], index, 0)
        moving = shifted(moving, "feat", -1)
        return (moving, stack)

    start = (panel, jnp.zeros((half, width, width), jnp.float32))
    opposite, grams = lax.fori_loop(0, half, advance, start)
    weight = shrink[0]
    scaled = grams / tokens * (1.0 - weight)
    local_trace = jnp.sum(jnp.diagonal(grams[0]) / tokens)
    mu = of_everyone(local_trace, "feat") / (width * lax.axis_size("feat"))
    members = (
        groups[:, None] == jnp.arange(group_scale.shape[1], dtype=jnp.int32)[None, :]
    ).astype(jnp.float32)
    gains = jnp.dot(members, group_scale[0], precision=lax.Precision.HIGHEST)
    diagonal = weight * mu * gains
    identity = jnp.eye(width, dtype=jnp.float32)
    factor = scaled.at[0].add(diagonal[:, None] * identity)
    lower = lax.axis_index("feat") < half
    rows_half = width // 2
    left = jnp.where(lower, panel[:, :rows_half], opposite[:, rows_half:])
    right = jnp.where(lower, opposite, panel)
    far = product(left, right) / tokens * (1.0 - weight)
    return (factor[None, None], far[None, None])


def solution(mesh):
    placed = (P(None, "layer", "feat"), P("layer", None), P("feat"), P("layer", None), P("layer"))
    return jax.shard_map(
        shards,
        mesh=mesh,
        in_specs=placed,
        out_specs=(P("layer", "feat", None, None, None), P("layer", "feat", None, None)),
        check_vma=False,
    )
```

profile of v0, /device:TPU:9, one launch (start us, length us, event | category | flops | bytes accessed | tf_op | source)
XLA Modules:
  0.0 347.2 jit_solution(15716076414738885085)
XLA Ops:
  3.7 7.2 %all-to-all-start = ((bf16[16,64,256]{2,1,0:T(8,128)(2,1)}), bf16[16,64,256]{2,1,0:T(8,128)(2,1)S(1)}, u32[]{:S(2)}, u32[]{:S(2)}) async-start(bf16[16,64,256]{2,1,0:T(8,128)(2,1)} %copy.15), calls=%async_computation | async-start | bytes 1048576 | tf_op jit(solution)/shard_map/all_to_all | solution.py:36
  12.5 9.7 %all-to-all-done = bf16[16,64,256]{2,1,0:T(8,128)(2,1)S(1)} async-done(((bf16[16,64,256]{2,1,0:T(8,128)(2,1)}), bf16[16,64,256]{2,1,0:T(8,128)(2,1)S(1)}, u32[]{:S(2)}, u32[]{:S(2)}) %all-to-all-start) | async-done | bytes 524320 | tf_op jit(solution)/shard_map/all_to_all | solution.py:36
  22.2 267.9 %while.16 = (s32[]{:T(128)}, bf16[1024,256]{1,0:T(8,128)(2,1)S(1)}, f32[16,256,256]{2,1,0:T(8,128)}, bf16[1024,256]{1,0:T(8,128)(2,1)S(1)}, s32[]{:T(128)}) while((s32[]{:T(128)}, bf16[1024,256]{1,0:T(8,128)(2,1)S(1)}, f32[16,256,256]{2,1,0:T(8,128)}, bf16[1024,256]{1,0:T(8,128)(2,1)S(1)}, s32[]{:T(128)}) %tuple.39), condition=%wide.region_1.0_spmd, body=%wide.region_0.0_spmd.sunk | while | flops 134217728 | bytes 4456561 | solution.py:49
  22.2 6.3 %collective-permute-start = (bf16[1024,256]{1,0:T(8,128)(2,1)S(1)}, bf16[1024,256]{1,0:T(8,128)(2,1)S(1)}, u32[]{:S(2)}, u32[]{:S(2)}) collective-permute-start(bf16[1024,256]{1,0:T(8,128)(2,1)S(1)} %copy.25), channel_id=1, source_target_pairs={{1,0},{2,1},{3,2},{4,3},{5,4},{6,5},{7,6},{8,7},{9,8},{10,9},{11,1... | collective-permute-start | bytes 1572872 | tf_op jit(solution)/shard_map/while/body/eval_jaxpr/ppermute | solution.py:10
  28.6 1.1 fusion.23
  29.6 14.2 %collective-permute-done = bf16[1024,256]{1,0:T(8,128)(2,1)S(1)} collective-permute-done((bf16[1024,256]{1,0:T(8,128)(2,1)S(1)}, bf16[1024,256]{1,0:T(8,128)(2,1)S(1)}, u32[]{:S(2)}, u32[]{:S(2)}) %collective-permute-start) | collective-permute-done | bytes 524320 | tf_op jit(solution)/shard_map/while/body/eval_jaxpr/ppermute | solution.py:10
  43.8 7.6 %collective-permute-start = (bf16[1024,256]{1,0:T(8,128)(2,1)S(1)}, bf16[1024,256]{1,0:T(8,128)(2,1)S(1)}, u32[]{:S(2)}, u32[]{:S(2)}) collective-permute-start(bf16[1024,256]{1,0:T(8,128)(2,1)S(1)} %copy.25), channel_id=1, source_target_pairs={{1,0},{2,1},{3,2},{4,3},{5,4},{6,5},{7,6},{8,7},{9,8},{10,9},{11,1... | collective-permute-start | bytes 1572872 | tf_op jit(solution)/shard_map/while/body/eval_jaxpr/ppermute | solution.py:10
  51.5 1.0 fusion.23
  52.5 7.4 %collective-permute-done = bf16[1024,256]{1,0:T(8,128)(2,1)S(1)} collective-permute-done((bf16[1024,256]{1,0:T(8,128)(2,1)S(1)}, bf16[1024,256]{1,0:T(8,128)(2,1)S(1)}, u32[]{:S(2)}, u32[]{:S(2)}) %collective-permute-start) | collective-permute-done | bytes 524320 | tf_op jit(solution)/shard_map/while/body/eval_jaxpr/ppermute | solution.py:10
  60.0 13.2 %collective-permute-start = (bf16[1024,256]{1,0:T(8,128)(2,1)S(1)}, bf16[1024,256]{1,0:T(8,128)(2,1)S(1)}, u32[]{:S(2)}, u32[]{:S(2)}) collective-permute-start(bf16[1024,256]{1,0:T(8,128)(2,1)S(1)} %copy.25), channel_id=1, source_target_pairs={{1,0},{2,1},{3,2},{4,3},{5,4},{6,5},{7,6},{8,7},{9,8},{10,9},{11,1... | collective-permute-start | bytes 1572872 | tf_op jit(solution)/shard_map/while/body/eval_jaxpr/ppermute | solution.py:10
  74.8 15.1 %collective-permute-start = (bf16[1024,256]{1,0:T(8,128)(2,1)S(1)}, bf16[1024,256]{1,0:T(8,128)(2,1)S(1)}, u32[]{:S(2)}, u32[]{:S(2)}) collective-permute-start(bf16[1024,256]{1,0:T(8,128)(2,1)S(1)} %copy.25), channel_id=1, source_target_pairs={{1,0},{2,1},{3,2},{4,3},{5,4},{6,5},{7,6},{8,7},{9,8},{10,9},{11,1... | collective-permute-start | bytes 1572872 | tf_op jit(solution)/shard_map/while/body/eval_jaxpr/ppermute | solution.py:10
  89.9 1.1 fusion.23
  91.4 15.0 %collective-permute-start = (bf16[1024,256]{1,0:T(8,128)(2,1)S(1)}, bf16[1024,256]{1,0:T(8,128)(2,1)S(1)}, u32[]{:S(2)}, u32[]{:S(2)}) collective-permute-start(bf16[1024,256]{1,0:T(8,128)(2,1)S(1)} %copy.25), channel_id=1, source_target_pairs={{1,0},{2,1},{3,2},{4,3},{5,4},{6,5},{7,6},{8,7},{9,8},{10,9},{11,1... | collective-permute-start | bytes 1572872 | tf_op jit(solution)/shard_map/while/body/eval_jaxpr/ppermute | solution.py:10
  106.4 1.0 fusion.23
  108.0 15.0 %collective-permute-start = (bf16[1024,256]{1,0:T(8,128)(2,1)S(1)}, bf16[1024,256]{1,0:T(8,128)(2,1)S(1)}, u32[]{:S(2)}, u32[]{:S(2)}) collective-permute-start(bf16[1024,256]{1,0:T(8,128)(2,1)S(1)} %copy.25), channel_id=1, source_target_pairs={{1,0},{2,1},{3,2},{4,3},{5,4},{6,5},{7,6},{8,7},{9,8},{10,9},{11,1... | collective-permute-start | bytes 1572872 | tf_op jit(solution)/shard_map/while/body/eval_jaxpr/ppermute | solution.py:10
  124.5 15.0 %collective-permute-start = (bf16[1024,256]{1,0:T(8,128)(2,1)S(1)}, bf16[1024,256]{1,0:T(8,128)(2,1)S(1)}, u32[]{:S(2)}, u32[]{:S(2)}) collective-permute-start(bf16[1024,256]{1,0:T(8,128)(2,1)S(1)} %copy.25), channel_id=1, source_target_pairs={{1,0},{2,1},{3,2},{4,3},{5,4},{6,5},{7,6},{8,7},{9,8},{10,9},{11,1... | collective-permute-start | bytes 1572872 | tf_op jit(solution)/shard_map/while/body/eval_jaxpr/ppermute | solution.py:10
  141.1 15.0 %collective-permute-start = (bf16[1024,256]{1,0:T(8,128)(2,1)S(1)}, bf16[1024,256]{1,0:T(8,128)(2,1)S(1)}, u32[]{:S(2)}, u32[]{:S(2)}) collective-permute-start(bf16[1024,256]{1,0:T(8,128)(2,1)S(1)} %copy.25), channel_id=1, source_target_pairs={{1,0},{2,1},{3,2},{4,3},{5,4},{6,5},{7,6},{8,7},{9,8},{10,9},{11,1... | collective-permute-start | bytes 1572872 | tf_op jit(solution)/shard_map/while/body/eval_jaxpr/ppermute | solution.py:10
  157.7 15.0 %collective-permute-start = (bf16[1024,256]{1,0:T(8,128)(2,1)S(1)}, bf16[1024,256]{1,0:T(8,128)(2,1)S(1)}, u32[]{:S(2)}, u32[]{:S(2)}) collective-permute-start(bf16[1024,256]{1,0:T(8,128)(2,1)S(1)} %copy.25), channel_id=1, source_target_pairs={{1,0},{2,1},{3,2},{4,3},{5,4},{6,5},{7,6},{8,7},{9,8},{10,9},{11,1... | collective-permute-start | bytes 1572872 | tf_op jit(solution)/shard_map/while/body/eval_jaxpr/ppermute | solution.py:10
  174.2 15.0 %collective-permute-start = (bf16[1024,256]{1,0:T(8,128)(2,1)S(1)}, bf16[1024,256]{1,0:T(8,128)(2,1)S(1)}, u32[]{:S(2)}, u32[]{:S(2)}) collective-permute-start(bf16[1024,256]{1,0:T(8,128)(2,1)S(1)} %copy.25), channel_id=1, source_target_pairs={{1,0},{2,1},{3,2},{4,3},{5,4},{6,5},{7,6},{8,7},{9,8},{10,9},{11,1... | collective-permute-start | bytes 1572872 | tf_op jit(solution)/shard_map/while/body/eval_jaxpr/ppermute | solution.py:10
  190.8 15.0 %collective-permute-start = (bf16[1024,256]{1,0:T(8,128)(2,1)S(1)}, bf16[1024,256]{1,0:T(8,128)(2,1)S(1)}, u32[]{:S(2)}, u32[]{:S(2)}) collective-permute-start(bf16[1024,256]{1,0:T(8,128)(2,1)S(1)} %copy.25), channel_id=1, source_target_pairs={{1,0},{2,1},{3,2},{4,3},{5,4},{6,5},{7,6},{8,7},{9,8},{10,9},{11,1... | collective-permute-start | bytes 1572872 | tf_op jit(solution)/shard_map/while/body/eval_jaxpr/ppermute | solution.py:10
  207.3 15.0 %collective-permute-start = (bf16[1024,256]{1,0:T(8,128)(2,1)S(1)}, bf16[1024,256]{1,0:T(8,128)(2,1)S(1)}, u32[]{:S(2)}, u32[]{:S(2)}) collective-permute-start(bf16[1024,256]{1,0:T(8,128)(2,1)S(1)} %copy.25), channel_id=1, source_target_pairs={{1,0},{2,1},{3,2},{4,3},{5,4},{6,5},{7,6},{8,7},{9,8},{10,9},{11,1... | collective-permute-start | bytes 1572872 | tf_op jit(solution)/shard_map/while/body/eval_jaxpr/ppermute | solution.py:10
  223.9 15.0 %collective-permute-start = (bf16[1024,256]{1,0:T(8,128)(2,1)S(1)}, bf16[1024,256]{1,0:T(8,128)(2,1)S(1)}, u32[]{:S(2)}, u32[]{:S(2)}) collective-permute-start(bf16[1024,256]{1,0:T(8,128)(2,1)S(1)} %copy.25), channel_id=1, source_target_pairs={{1,0},{2,1},{3,2},{4,3},{5,4},{6,5},{7,6},{8,7},{9,8},{10,9},{11,1... | collective-permute-start | bytes 1572872 | tf_op jit(solution)/shard_map/while/body/eval_jaxpr/ppermute | solution.py:10
  240.4 15.0 %collective-permute-start = (bf16[1024,256]{1,0:T(8,128)(2,1)S(1)}, bf16[1024,256]{1,0:T(8,128)(2,1)S(1)}, u32[]{:S(2)}, u32[]{:S(2)}) collective-permute-start(bf16[1024,256]{1,0:T(8,128)(2,1)S(1)} %copy.25), channel_id=1, source_target_pairs={{1,0},{2,1},{3,2},{4,3},{5,4},{6,5},{7,6},{8,7},{9,8},{10,9},{11,1... | collective-permute-start | bytes 1572872 | tf_op jit(solution)/shard_map/while/body/eval_jaxpr/ppermute | solution.py:10
  257.0 15.0 %collective-permute-start = (bf16[1024,256]{1,0:T(8,128)(2,1)S(1)}, bf16[1024,256]{1,0:T(8,128)(2,1)S(1)}, u32[]{:S(2)}, u32[]{:S(2)}) collective-permute-start(bf16[1024,256]{1,0:T(8,128)(2,1)S(1)} %copy.25), channel_id=1, source_target_pairs={{1,0},{2,1},{3,2},{4,3},{5,4},{6,5},{7,6},{8,7},{9,8},{10,9},{11,1... | collective-permute-start | bytes 1572872 | tf_op jit(solution)/shard_map/while/body/eval_jaxpr/ppermute | solution.py:10
  273.5 15.0 %collective-permute-start = (bf16[1024,256]{1,0:T(8,128)(2,1)S(1)}, bf16[1024,256]{1,0:T(8,128)(2,1)S(1)}, u32[]{:S(2)}, u32[]{:S(2)}) collective-permute-start(bf16[1024,256]{1,0:T(8,128)(2,1)S(1)} %copy.25), channel_id=1, source_target_pairs={{1,0},{2,1},{3,2},{4,3},{5,4},{6,5},{7,6},{8,7},{9,8},{10,9},{11,1... | collective-permute-start | bytes 1572872 | tf_op jit(solution)/shard_map/while/body/eval_jaxpr/ppermute | solution.py:10
  291.0 4.6 %broadcast_multiply_fusion = f32[16,256,256]{2,1,0:T(8,128)} fusion(f32[16,256,256]{2,1,0:T(8,128)} %get-tuple-element.94, f32[]{:T(128)S(6)} %mul.31), kind=kLoop, calls=%fused_computation.3 | loop fusion | flops 1048576 | bytes 8388612 | tf_op jit(solution)/shard_map/mul | solution.py:51
  295.7 2.5 fusion.17
  298.2 2.3 gather_fusion
  301.1 1.3 broadcast_in_dim.31
  302.4 30.1 %all-to-all-start.1 = ((f32[32,1,1]{2,1,0:T(1,128)}), f32[32,1,1]{2,1,0:T(1,128)S(1)}, u32[]{:S(2)}, u32[]{:S(2)}) async-start(f32[32,1,1]{2,1,0:T(1,128)} %broadcast_in_dim.31), calls=%async_computation.1 | async-start | bytes 32768 | tf_op jit(solution)/shard_map/all_to_all | solution.py:15
  333.4 10.8 %all-to-all-done.1 = f32[32,1,1]{2,1,0:T(1,128)S(1)} async-done(((f32[32,1,1]{2,1,0:T(1,128)}), f32[32,1,1]{2,1,0:T(1,128)S(1)}, u32[]{:S(2)}, u32[]{:S(2)}) %all-to-all-start.1) | async-done | bytes 160 | tf_op jit(solution)/shard_map/all_to_all | solution.py:15
  345.4 1.8 fusion.6
  (57 shorter events, 26.8 us)
Async XLA Ops:
  0.6 1.0 copy-start
  3.7 18.5 %all-to-all-start = ((bf16[16,64,256]{2,1,0:T(8,128)(2,1)}), bf16[16,64,256]{2,1,0:T(8,128)(2,1)S(1)}, u32[]{:S(2)}, u32[]{:S(2)}) async-start(bf16[16,64,256]{2,1,0:T(8,128)(2,1)} %copy.15), calls=%async_computation | async-start | bytes 1048576 | tf_op jit(solution)/shard_map/all_to_all | solution.py:36
  22.2 21.5 %collective-permute-start = (bf16[1024,256]{1,0:T(8,128)(2,1)S(1)}, bf16[1024,256]{1,0:T(8,128)(2,1)S(1)}, u32[]{:S(2)}, u32[]{:S(2)}) collective-permute-start(bf16[1024,256]{1,0:T(8,128)(2,1)S(1)} %copy.25), channel_id=1, source_target_pairs={{1,0},{2,1},{3,2},{4,3},{5,4},{6,5},{7,6},{8,7},{9,8},{10,9},{11,1... | collective-permute-start | bytes 1572872 | tf_op jit(solution)/shard_map/while/body/eval_jaxpr/ppermute | solution.py:10
  43.8 16.1 %collective-permute-start = (bf16[1024,256]{1,0:T(8,128)(2,1)S(1)}, bf16[1024,256]{1,0:T(8,128)(2,1)S(1)}, u32[]{:S(2)}, u32[]{:S(2)}) collective-permute-start(bf16[1024,256]{1,0:T(8,128)(2,1)S(1)} %copy.25), channel_id=1, source_target_pairs={{1,0},{2,1},{3,2},{4,3},{5,4},{6,5},{7,6},{8,7},{9,8},{10,9},{11,1... | collective-permute-start | bytes 1572872 | tf_op jit(solution)/shard_map/while/body/eval_jaxpr/ppermute | solution.py:10
  60.0 14.8 %collective-permute-start = (bf16[1024,256]{1,0:T(8,128)(2,1)S(1)}, bf16[1024,256]{1,0:T(8,128)(2,1)S(1)}, u32[]{:S(2)}, u32[]{:S(2)}) collective-permute-start(bf16[1024,256]{1,0:T(8,128)(2,1)S(1)} %copy.25), channel_id=1, source_target_pairs={{1,0},{2,1},{3,2},{4,3},{5,4},{6,5},{7,6},{8,7},{9,8},{10,9},{11,1... | collective-permute-start | bytes 1572872 | tf_op jit(solution)/shard_map/while/body/eval_jaxpr/ppermute | solution.py:10
  74.8 16.6 %collective-permute-start = (bf16[1024,256]{1,0:T(8,128)(2,1)S(1)}, bf16[1024,256]{1,0:T(8,128)(2,1)S(1)}, u32[]{:S(2)}, u32[]{:S(2)}) collective-permute-start(bf16[1024,256]{1,0:T(8,128)(2,1)S(1)} %copy.25), channel_id=1, source_target_pairs={{1,0},{2,1},{3,2},{4,3},{5,4},{6,5},{7,6},{8,7},{9,8},{10,9},{11,1... | collective-permute-start | bytes 1572872 | tf_op jit(solution)/shard_map/while/body/eval_jaxpr/ppermute | solution.py:10
  91.4 16.5 %collective-permute-start = (bf16[1024,256]{1,0:T(8,128)(2,1)S(1)}, bf16[1024,256]{1,0:T(8,128)(2,1)S(1)}, u32[]{:S(2)}, u32[]{:S(2)}) collective-permute-start(bf16[1024,256]{1,0:T(8,128)(2,1)S(1)} %copy.25), channel_id=1, source_target_pairs={{1,0},{2,1},{3,2},{4,3},{5,4},{6,5},{7,6},{8,7},{9,8},{10,9},{11,1... | collective-permute-start | bytes 1572872 | tf_op jit(solution)/shard_map/while/body/eval_jaxpr/ppermute | solution.py:10
  108.0 16.5 %collective-permute-start = (bf16[1024,256]{1,0:T(8,128)(2,1)S(1)}, bf16[1024,256]{1,0:T(8,128)(2,1)S(1)}, u32[]{:S(2)}, u32[]{:S(2)}) collective-permute-start(bf16[1024,256]{1,0:T(8,128)(2,1)S(1)} %copy.25), channel_id=1, source_target_pairs={{1,0},{2,1},{3,2},{4,3},{5,4},{6,5},{7,6},{8,7},{9,8},{10,9},{11,1... | collective-permute-start | bytes 1572872 | tf_op jit(solution)/shard_map/while/body/eval_jaxpr/ppermute | solution.py:10
  124.5 16.5 %collective-permute-start = (bf16[1024,256]{1,0:T(8,128)(2,1)S(1)}, bf16[1024,256]{1,0:T(8,128)(2,1)S(1)}, u32[]{:S(2)}, u32[]{:S(2)}) collective-permute-start(bf16[1024,256]{1,0:T(8,128)(2,1)S(1)} %copy.25), channel_id=1, source_target_pairs={{1,0},{2,1},{3,2},{4,3},{5,4},{6,5},{7,6},{8,7},{9,8},{10,9},{11,1... | collective-permute-start | bytes 1572872 | tf_op jit(solution)/shard_map/while/body/eval_jaxpr/ppermute | solution.py:10
  141.1 16.5 %collective-permute-start = (bf16[1024,256]{1,0:T(8,128)(2,1)S(1)}, bf16[1024,256]{1,0:T(8,128)(2,1)S(1)}, u32[]{:S(2)}, u32[]{:S(2)}) collective-permute-start(bf16[1024,256]{1,0:T(8,128)(2,1)S(1)} %copy.25), channel_id=1, source_target_pairs={{1,0},{2,1},{3,2},{4,3},{5,4},{6,5},{7,6},{8,7},{9,8},{10,9},{11,1... | collective-permute-start | bytes 1572872 | tf_op jit(solution)/shard_map/while/body/eval_jaxpr/ppermute | solution.py:10
  157.7 16.5 %collective-permute-start = (bf16[1024,256]{1,0:T(8,128)(2,1)S(1)}, bf16[1024,256]{1,0:T(8,128)(2,1)S(1)}, u32[]{:S(2)}, u32[]{:S(2)}) collective-permute-start(bf16[1024,256]{1,0:T(8,128)(2,1)S(1)} %copy.25), channel_id=1, source_target_pairs={{1,0},{2,1},{3,2},{4,3},{5,4},{6,5},{7,6},{8,7},{9,8},{10,9},{11,1... | collective-permute-start | bytes 1572872 | tf_op jit(solution)/shard_map/while/body/eval_jaxpr/ppermute | solution.py:10
  174.2 16.5 %collective-permute-start = (bf16[1024,256]{1,0:T(8,128)(2,1)S(1)}, bf16[1024,256]{1,0:T(8,128)(2,1)S(1)}, u32[]{:S(2)}, u32[]{:S(2)}) collective-permute-start(bf16[1024,256]{1,0:T(8,128)(2,1)S(1)} %copy.25), channel_id=1, source_target_pairs={{1,0},{2,1},{3,2},{4,3},{5,4},{6,5},{7,6},{8,7},{9,8},{10,9},{11,1... | collective-permute-start | bytes 1572872 | tf_op jit(solution)/shard_map/while/body/eval_jaxpr/ppermute | solution.py:10
  190.8 16.5 %collective-permute-start = (bf16[1024,256]{1,0:T(8,128)(2,1)S(1)}, bf16[1024,256]{1,0:T(8,128)(2,1)S(1)}, u32[]{:S(2)}, u32[]{:S(2)}) collective-permute-start(bf16[1024,256]{1,0:T(8,128)(2,1)S(1)} %copy.25), channel_id=1, source_target_pairs={{1,0},{2,1},{3,2},{4,3},{5,4},{6,5},{7,6},{8,7},{9,8},{10,9},{11,1... | collective-permute-start | bytes 1572872 | tf_op jit(solution)/shard_map/while/body/eval_jaxpr/ppermute | solution.py:10
  207.3 16.5 %collective-permute-start = (bf16[1024,256]{1,0:T(8,128)(2,1)S(1)}, bf16[1024,256]{1,0:T(8,128)(2,1)S(1)}, u32[]{:S(2)}, u32[]{:S(2)}) collective-permute-start(bf16[1024,256]{1,0:T(8,128)(2,1)S(1)} %copy.25), channel_id=1, source_target_pairs={{1,0},{2,1},{3,2},{4,3},{5,4},{6,5},{7,6},{8,7},{9,8},{10,9},{11,1... | collective-permute-start | bytes 1572872 | tf_op jit(solution)/shard_map/while/body/eval_jaxpr/ppermute | solution.py:10
  223.9 16.5 %collective-permute-start = (bf16[1024,256]{1,0:T(8,128)(2,1)S(1)}, bf16[1024,256]{1,0:T(8,128)(2,1)S(1)}, u32[]{:S(2)}, u32[]{:S(2)}) collective-permute-start(bf16[1024,256]{1,0:T(8,128)(2,1)S(1)} %copy.25), channel_id=1, source_target_pairs={{1,0},{2,1},{3,2},{4,3},{5,4},{6,5},{7,6},{8,7},{9,8},{10,9},{11,1... | collective-permute-start | bytes 1572872 | tf_op jit(solution)/shard_map/while/body/eval_jaxpr/ppermute | solution.py:10
  240.4 16.5 %collective-permute-start = (bf16[1024,256]{1,0:T(8,128)(2,1)S(1)}, bf16[1024,256]{1,0:T(8,128)(2,1)S(1)}, u32[]{:S(2)}, u32[]{:S(2)}) collective-permute-start(bf16[1024,256]{1,0:T(8,128)(2,1)S(1)} %copy.25), channel_id=1, source_target_pairs={{1,0},{2,1},{3,2},{4,3},{5,4},{6,5},{7,6},{8,7},{9,8},{10,9},{11,1... | collective-permute-start | bytes 1572872 | tf_op jit(solution)/shard_map/while/body/eval_jaxpr/ppermute | solution.py:10
  257.0 16.5 %collective-permute-start = (bf16[1024,256]{1,0:T(8,128)(2,1)S(1)}, bf16[1024,256]{1,0:T(8,128)(2,1)S(1)}, u32[]{:S(2)}, u32[]{:S(2)}) collective-permute-start(bf16[1024,256]{1,0:T(8,128)(2,1)S(1)} %copy.25), channel_id=1, source_target_pairs={{1,0},{2,1},{3,2},{4,3},{5,4},{6,5},{7,6},{8,7},{9,8},{10,9},{11,1... | collective-permute-start | bytes 1572872 | tf_op jit(solution)/shard_map/while/body/eval_jaxpr/ppermute | solution.py:10
  273.5 16.5 %collective-permute-start = (bf16[1024,256]{1,0:T(8,128)(2,1)S(1)}, bf16[1024,256]{1,0:T(8,128)(2,1)S(1)}, u32[]{:S(2)}, u32[]{:S(2)}) collective-permute-start(bf16[1024,256]{1,0:T(8,128)(2,1)S(1)} %copy.25), channel_id=1, source_target_pairs={{1,0},{2,1},{3,2},{4,3},{5,4},{6,5},{7,6},{8,7},{9,8},{10,9},{11,1... | collective-permute-start | bytes 1572872 | tf_op jit(solution)/shard_map/while/body/eval_jaxpr/ppermute | solution.py:10
  291.0 4.6 %copy-start.1 = (f32[16,256,256]{2,1,0:T(8,128)S(1)}, f32[16,256,256]{2,1,0:T(8,128)}, u32[]{:S(2)}) copy-start(f32[16,256,256]{2,1,0:T(8,128)} %get-tuple-element.94) | copy-start | bytes 12582916
  302.4 41.8 %all-to-all-start.1 = ((f32[32,1,1]{2,1,0:T(1,128)}), f32[32,1,1]{2,1,0:T(1,128)S(1)}, u32[]{:S(2)}, u32[]{:S(2)}) async-start(f32[32,1,1]{2,1,0:T(1,128)} %broadcast_in_dim.31), calls=%async_computation.1 | async-start | bytes 32768 | tf_op jit(solution)/shard_map/all_to_all | solution.py:15
where the time goes:
time: 349 us; the launch traced here: 347 us
  starting transfers between devices  260 us (74%)
  waiting for transfers between devices  48.6 us (14%)
  matrix products  19.6 us (6%)
  other arithmetic  10.1 us (3%)
  local copies, waits for them, and re-layouts  7.16 us (2%)
    ppermute x16, starting transfers between devices, shifted(): return lax.ppermute(block, axis, route)  222 us
    all_to_all x1, starting transfers between devices, copy_for_each(): return lax.all_to_all(copies, axis, split_axis=0, concat_axis=0, tiled=True)  30.1 us
    ppermute x16, waiting for transfers between devices, shifted(): return lax.ppermute(block, axis, route)  28.2 us
    dot_general x17, matrix products, product(): lax.dot_general(left, right, (((0,), (0,)), ((), ())), preferred_element_...  17.7 us
    all_to_all x1, waiting for transfers between devices, copy_for_each(): return lax.all_to_all(copies, axis, split_axis=0, concat_axis=0, tiled=True)  10.8 us
    all_to_all x1, waiting for transfers between devices, shards(): lax.all_to_all(ordered, 'layer', split_axis=0, concat_axis=1, tiled=True)  9.67 us
    all_to_all x1, starting transfers between devices, shards(): lax.all_to_all(ordered, 'layer', split_axis=0, concat_axis=1, tiled=True)  7.24 us
  transfers between devices with their start and end apart: 18, of which 18 were waited for; matrix products, arithmetic and copies ran while one was open for 5% of the time, Pallas kernels for 0%

commit v1 on v0

v1 whole, which is shorter than its diff:
```python
import jax
import jax.numpy as jnp
from jax import lax
from jax.experimental import pallas as pl
from jax.experimental.pallas import tpu as pltpu
from jax.sharding import PartitionSpec as P

X, YLO, YHI, Z, CORES = 4, 4, 2, 8, 2
BLOCKS = X * YLO
ROWS = 64
WIDTH = 256
TOKENS = BLOCKS * ROWS
FEATURES = WIDTH * Z * YHI * CORES
GROUPED = 4
CROSS_LAG = 2
ALL_HERE = 6
STEPS = 26
OFFSETS = [(dx, dy) for dy in (0, 1, 3, 2) for dx in (0, 1, 3, 2)]
F32 = jnp.float32


def product(left, right):
    return jnp.dot(left, right, preferred_element_type=F32)


def kernel(
    acts, order, groups, group_scale, shrink,
    out, far,
    outgoing, own, oth, sib, flipped, parts, sib_parts,
    a_send, a_recv, own_send, own_recv, cross_send, oth_send, oth_recv,
    sib_send, sib_recv, part_send, part_recv, partx_send, partx_recv, parts_send, parts_recv,
):
    layer = lax.axis_index("layer")
    feat = lax.axis_index("feat")
    x, ylo = layer // YLO, layer % YLO
    z, high, core = feat // (YHI * CORES), (feat // CORES) % YHI, feat % CORES

    def at(dz, other_high=False, other_core=False):
        zz = (z + dz + Z) % Z
        hh = 1 - high if other_high else high
        cc = 1 - core if other_core else core
        return (layer, zz * (YHI * CORES) + hh * CORES + cc)

    def peer(dx, dy):
        return (((x + dx) % X) * YLO + (ylo + dy) % YLO, feat)

    down, up, across, sibling = at(-1), at(1), at(0, True), at(0, False, True)

    def remote(src, dst, send, recv, device):
        return pltpu.make_async_remote_copy(
            src_ref=src, dst_ref=dst, send_sem=send, recv_sem=recv,
            device_id=device, device_id_type=pl.DeviceIdType.MESH,
        )

    barrier = pltpu.get_barrier_semaphore()
    partners = [peer(dx, dy) for dx, dy in OFFSETS[1:]] + [down, up, across, sibling]
    for device in partners:
        pl.semaphore_signal(
            barrier, inc=1, device_id=device, device_id_type=pl.DeviceIdType.MESH
        )

    def slot_of(target):
        slot = jnp.int32(0)
        for j in range(BLOCKS):
            slot = jnp.where(order[0, j] == target, j, slot)
        return slot

    for i, (dx, dy) in enumerate(OFFSETS):
        block = acts[slot_of(peer(dx, dy)[0])]
        if i == 0:
            own[0, 0] = block
        else:
            outgoing[i - 1] = block

    def clear(k, carry):
        out[k] = jnp.zeros((WIDTH, WIDTH), F32)
        return carry

    lax.fori_loop(0, 16, clear, 0)
    far[...] = jnp.zeros((WIDTH // 2, WIDTH), F32)
    pl.semaphore_wait(barrier, len(partners))

    scale = (1.0 - shrink[0]) * (1.0 / TOKENS)

    def landing(i):
        dx, dy = OFFSETS[i]
        return OFFSETS.index(((-dx) % X, (-dy) % YLO))

    def first_copy(i):
        to = landing(i)
        return remote(
            outgoing.at[i - 1], own.at[0, to], a_send, a_recv.at[to], peer(*OFFSETS[i])
        )

    for i in range(1, BLOCKS):
        first_copy(i).start()

    def first_arrival(b):
        remote(own.at[0, b], own.at[0, b], a_send, a_recv.at[b], sibling).wait_recv()

    def grouped(ref, slot, q):
        return ref[slot, pl.ds(q * GROUPED, GROUPED)].reshape(GROUPED * ROWS, WIDTH)

    def flipped_group(q):
        return flipped[:, pl.ds(pl.multiple_of(q * GROUPED * ROWS, GROUPED * ROWS), GROUPED * ROWS)]

    def finished(total, q):
        return total * jnp.where(q == BLOCKS // GROUPED - 1, scale, 1.0)

    def accumulate(k, panel, q):
        out[k] = finished(out[k] + product(flipped_group(q), panel), q)

    lower = z < Z // 2

    def accumulate_far(q):
        mine, opposite = grouped(own, 0, q), grouped(own, 4, q)
        half = WIDTH // 2
        left = jnp.where(lower, mine[:, :half], opposite[:, half:])
        right = jnp.where(lower, opposite, mine)
        term = lax.dot_general(
            left, right, (((0,), (0,)), ((), ())), preferred_element_type=F32
        )
        far[...] = finished(far[...] + term, q)

    def to_sibling(ref, slot, place, q):
        part = pl.ds(q * GROUPED, GROUPED)
        remote(
            ref.at[slot, part], sib.at[place, part], sib_send, sib_recv.at[place, q], sibling
        ).start()

    def inside(b):
        return (b >= 0) & (b < BLOCKS)

    def ends_group(b):
        return inside(b) & (b % GROUPED == GROUPED - 1)

    def step(t, carry):
        @pl.when(t < BLOCKS)
        def _():
            @pl.when((t > 0) & (t <= ALL_HERE))
            def _():
                first_arrival(t)

            remote(
                own.at[0, t], own.at[1, t], own_send, own_recv.at[1, t], down
            ).start()

        for d in range(1, 5):
            b = t - d

            @pl.when(inside(b))
            def _(d=d, b=b):
                remote(
                    own.at[d, b], own.at[d, b], own_send, own_recv.at[d, b], down
                ).wait_recv()
                if d < 4:
                    remote(
                        own.at[d, b], own.at[d + 1, b], own_send, own_recv.at[d + 1, b], down
                    ).start()
                if d >= 3:
                    @pl.when(high == 4 - d)
                    def _():
                        remote(
                            own.at[d, b], oth.at[0, b], cross_send, oth_recv.at[0, b], across
                        ).start()

        first = 3 + high + CROSS_LAG
        for o in range(4):
            b = t - first - o

            @pl.when(inside(b))
            def _(o=o, b=b):
                remote(
                    oth.at[o, b], oth.at[o, b], oth_send, oth_recv.at[o, b], up
                ).wait_recv()
                if o < 3:
                    remote(
                        oth.at[o, b], oth.at[o + 1, b], oth_send, oth_recv.at[o + 1, b], up
                    ).start()

        for d in range(5):
            b = t - d
            place = d - 1 + core

            @pl.when(ends_group(b) & (place >= 0) & (place < 4))
            def _(d=d, b=b, place=place):
                to_sibling(own, d, place, b // GROUPED)

        for o in range(4):
            b = t - first - o

            @pl.when(ends_group(b))
            def _(o=o, b=b):
                to_sibling(oth, o, 4 + o, b // GROUPED)

        @pl.when(t == ALL_HERE)
        def _():
            for b in range(ALL_HERE + 1, BLOCKS):
                first_arrival(b)

            def add(b, total):
                values = own[0, b].astype(F32)
                squares = (values * values).reshape(ROWS // 8, 8, WIDTH).sum(axis=0)
                return total + squares[:, :128] + squares[:, 128:]

            parts[0, 0] = lax.fori_loop(0, BLOCKS, add, jnp.zeros((8, 128), F32))

        ring = t - (ALL_HERE + 1)

        @pl.when((ring >= 1) & (ring < Z))
        def _():
            remote(
                parts.at[0, ring], parts.at[0, ring], part_send, part_recv.at[ring], down
            ).wait_recv()

        @pl.when((ring >= 0) & (ring < Z - 1))
        def _():
            remote(
                parts.at[0, ring], parts.at[0, ring + 1], part_send, part_recv.at[ring + 1], down
            ).start()

        crossing = remote(parts.at[0], parts.at[1], partx_send, partx_recv, across)
        sharing = remote(parts, sib_parts, parts_send, parts_recv, sibling)

        @pl.when(ring == Z - 1)
        def _():
            crossing.start()

        @pl.when(ring == Z + 1)
        def _():
            crossing.wait()
            sharing.start()

        @pl.when(ring == Z + 2)
        def _():
            sharing.wait()
            trace = jnp.sum(parts[...]) + jnp.sum(sib_parts[...])
            mu = trace * (1.0 / TOKENS / FEATURES)

            def gain_of(g, gains):
                return jnp.where(groups[...] == g, group_scale[0, g], gains)

            gains = lax.fori_loop(
                0, group_scale.shape[1], gain_of, jnp.zeros((1, WIDTH), F32)
            )
            rows = lax.broadcasted_iota(jnp.int32, (WIDTH, WIDTH), 0)
            columns = lax.broadcasted_iota(jnp.int32, (WIDTH, WIDTH), 1)
            out[0] = out[0] + jnp.where(rows == columns, shrink[0] * mu * gains, 0.0)

        @pl.when((t < BLOCKS) & (t % GROUPED == GROUPED - 1))
        def _():
            q = t // GROUPED
            panel = grouped(own, 0, q)
            flipped[:, pl.ds(pl.multiple_of(q * GROUPED * ROWS, GROUPED * ROWS), GROUPED * ROWS)] = panel.T
            accumulate(0, panel, q)

        for d in range(1, 5):
            b = t - d

            @pl.when(ends_group(b))
            def _(d=d, b=b):
                q = b // GROUPED
                if d < 4:
                    accumulate(4 * d, grouped(own, d, q), q)
                else:
                    accumulate_far(q)

        for o in range(4):
            b = t - first - o

            @pl.when(ends_group(b))
            def _(o=o, b=b):
                q = b // GROUPED
                accumulate(14 - 4 * o, grouped(oth, o, q), q)

        for place in range(8):
            if place < 4:
                b = t - 1 - (place + core)
                k = 4 * place + 1 + 2 * core
            else:
                b = t - 1 - first - (place - 4)
                k = 15 - 4 * (place - 4) - 2 * core

            @pl.when(ends_group(b))
            def _(place=place, b=b, k=k):
                q = b // GROUPED
                part = pl.ds(q * GROUPED, GROUPED)
                remote(
                    sib.at[place, part], sib.at[place, part], sib_send,
                    sib_recv.at[place, q], sibling,
                ).wait_recv()
                accumulate(k, grouped(sib, place, q), q)

        return carry

    lax.fori_loop(0, STEPS, step, 0)

    def sent(ref, sem):
        remote(ref, ref, sem, sem, sibling).wait_send()

    sent(outgoing, a_send)
    sent(own.at[pl.ds(0, 4)], own_send)
    sent(oth.at[0], cross_send)
    sent(oth.at[pl.ds(0, 3)], oth_send)
    sent(sib, sib_send)
    sent(parts.at[0, pl.ds(0, Z - 1)], part_send)


def shards(acts, layer_order, groups, group_scale, shrink):
    vmem = pl.BlockSpec(memory_space=pltpu.VMEM)
    smem = pl.BlockSpec(memory_space=pltpu.SMEM)
    dma = pltpu.SemaphoreType.DMA
    bf16 = jnp.bfloat16
    factor, far = pl.pallas_call(
        kernel,
        out_shape=(
            jax.ShapeDtypeStruct((16, WIDTH, WIDTH), F32),
            jax.ShapeDtypeStruct((WIDTH // 2, WIDTH), F32),
        ),
        in_specs=[vmem, smem, vmem, smem, smem],
        out_specs=(vmem, vmem),
        scratch_shapes=[
            pltpu.VMEM((BLOCKS - 1, ROWS, WIDTH), bf16),
            pltpu.VMEM((5, BLOCKS, ROWS, WIDTH), bf16),
            pltpu.VMEM((4, BLOCKS, ROWS, WIDTH), bf16),
            pltpu.VMEM((8, BLOCKS, ROWS, WIDTH), bf16),
            pltpu.VMEM((WIDTH, TOKENS), bf16),
            pltpu.VMEM((2, Z, 8, 128), F32),
            pltpu.VMEM((2, Z, 8, 128), F32),
            dma, dma((BLOCKS,)), dma, dma((5, BLOCKS)), dma, dma, dma((4, BLOCKS)),
            dma, dma((8, BLOCKS // GROUPED)), dma, dma((Z,)), dma, dma, dma, dma,
        ],
        compiler_params=pltpu.CompilerParams(
            collective_id=0, has_side_effects=True, vmem_limit_bytes=40 * 1024 * 1024
        ),
        name="gram",
    )(acts, layer_order, groups[None, :], group_scale, shrink)
    return (factor[None, None], far[None, None])


def solution(mesh):
    placed = (P(None, "layer", "feat"), P("layer", None), P("feat"), P("layer", None), P("layer"))
    return jax.shard_map(
        shards,
        mesh=mesh,
        in_specs=placed,
        out_specs=(P("layer", "feat", None, None, None), P("layer", "feat", None, None)),
        check_vma=False,
    )
```

time: 349 us -> 106 us (0.30)
  the two profiles are of different devices: /device:TPU:9 before, /device:TPU:1 now
where the time goes in v1:
time: 106 us; the launch traced here: 105 us
  Pallas kernels  98.4 us (93%)
  local copies, waits for them, and re-layouts  5.69 us (5%)
  between operations  1.3 us (1%)
    pallas_call x1, Pallas kernels, shards(): pl.pallas_call(kernel, out_shape=(jax.ShapeDtypeStruct((16, WIDTH, WIDTH)...  98.4 us
    unnamed x10, local copies, waits for them, and re-layouts  5.69 us

profile of v1, /device:TPU:1, one launch (start us, length us, event | category | flops | bytes accessed | tf_op | source)
XLA Modules:
  0.0 105.4 jit_solution(9053597962431089785)
XLA Ops:
  1.3 0.0 copy-start
  1.3 1.0 copy-done
  2.3 0.0 copy-start.1
  2.3 0.7 copy-done.1
  3.0 0.0 copy-start.2
  3.0 0.7 copy-done.2
  3.7 0.0 copy-start.3
  3.7 0.7 copy-done.3
  4.3 98.4 %gram.1 = (f32[16,256,256]{2,1,0:T(8,128)S(1)}, f32[128,256]{1,0:T(8,128)S(1)}) custom-call(bf16[16,64,256]{2,1,0:T(8,128)(2,1)S(1)} %copy-done, s32[1,16]{1,0:T(1,128)S(1)} %copy-done.2, s32[1,256]{1,0:T(1,128)S(1)} %bitcast.5, f32[1,64]{1,0:T(1,128)S(1)} %copy-done.3, f32[1]{0:T(128)S(6)} %copy.9.shrink), custom_call_target="tpu_custom_call" | custom-call | tf_op jit(solution)/shard_map/gram/pallas_call | solution.py:314
  102.7 2.0 %copy.10 = f32[1,1,16,256,256]{4,3,2,1,0:T(8,128)} copy(f32[1,1,16,256,256]{4,3,2,1,0:T(8,128)S(1)} %bitcast.3) | data formatting | bytes 8388608
  104.7 0.7 copy.11
Async XLA Ops:
  1.3 1.0 copy-start
  2.3 0.7 copy-start.1
  3.0 0.7 copy-start.2
  3.7 0.7 copy-start.3
